TPU v7x, 128 devices: a whole 4x4x4 slice. The times are simulated.
128 devices in a mesh: layer: 2 (over core), expert: 16 (over y, x), matrix: 4 (over z).
Axes of the slice: x: 4, y: 4, z: 4, core: 2. Of those that a mesh axis runs over, the one named last changes fastest.
Arguments:
- grads: float32 [32, 1, 2048, 768], P(('layer', 'expert'), None, 'matrix'), parts along dimension 0, may hold values from -6 to 6
- basis_out: float32 [32, 2048, 2048], P('layer', None, ('expert', 'matrix')), parts along dimension 0, may hold values from -0.125 to 0.125
- basis_in: float32 [32, 768, 768], P('layer', ('expert', 'matrix')), parts along dimension 0, may hold values from -0.21875 to 0.21875
- eigvals: float32 [32, 2048, 768], P('layer', ('expert', 'matrix')), parts along dimension 0, may hold values from 0.001 to 1
- counts: int32 [32], P(('layer', 'expert')), parts along dimension 0, may hold values from 0 to 1, as said below
- slot_query: int32 [32, 1], P(('layer', 'expert')), parts along dimension 0, may hold values from 0 to 31
Outputs:
- precond: float32 [32, 1, 2048, 768], P(('layer', 'expert'), None, 'matrix'), parts along dimension 0
- scores: float32 [64], P('layer'), parts along dimension 0
There are 2 independent parts, one for each index of `layer`. A program takes and returns all parts, laid end to end along the dimension named above; each array names one. Nothing has to cross between parts.
Inputs may be any that keep to these rules, and one draw needn't show every extreme that they name: `counts`: some expert has no live slot and some expert has all 1.
All inputs are finite; a program needn't handle non-finite values.
Results may differ from a plain program's by a relative error of at most 0.0003.
Values sent between devices are 32-bit elements; how exact they have to be, the bound alone decides.
A program may use at most 64 MiB of HBM per device.

v0:
```python
import jax
import jax.numpy as jnp
from jax import lax
from jax.sharding import PartitionSpec as P

QUERIES = 32
damping_fixed = 0.05
highest = lax.Precision.HIGHEST


def shards(grads, basis_out, basis_in, eigvals, counts, slot_query):
    capacity = grads.shape[1]
    own_rows = grads.shape[2]
    in_width = grads.shape[3]
    groups = lax.axis_size("matrix")
    columns = lax.all_to_all(basis_out, "expert", split_axis=0, concat_axis=2, tiled=True)[0]
    scales, inner = (
        lax.all_to_all(eigvals, "expert", split_axis=0, concat_axis=1, tiled=True),
        lax.all_to_all(basis_in, "expert", split_axis=0, concat_axis=1, tiled=True),
    )
    inner = lax.all_gather(inner, "matrix", axis=1, tiled=True)[0]
    sources = lax.axis_size("expert")
    inner = inner.reshape(groups, sources, -1, in_width).transpose(1, 0, 2, 3).reshape(-1, in_width)
    divisor = scales[0] + damping_fixed
    live_count = counts[0]
    queries = slot_query[0]
    local_rows = grads[0]
    slot_ids = jnp.arange(capacity, dtype=jnp.int32)
    live = (slot_ids < live_count).astype(jnp.float32)
    rotated = jnp.einsum(
        "ik,if->kf",
        columns,
        lax.all_gather(local_rows[0], "matrix", axis=0, tiled=True),
        precision=highest,
    )
    rotated = jnp.dot(rotated, inner, precision=highest)
    scaled = rotated / divisor
    back = jnp.einsum("kg,hg->kh", scaled, inner, precision=highest)

    def project_one(start, amount, back=back):
        return jnp.dot(columns, back, precision=highest)

    result = lax.psum_scatter(
        project_one(jnp.int32(0), own_rows * lax.axis_size("matrix")),
        "matrix",
        scatter_dimension=0,
        tiled=True,
    )
    results = [result * live[0]]
    precond = jnp.stack(results)
    values = jnp.sum(local_rows * precond, axis=(1, 2)) / (own_rows * groups * in_width)
    targets = jnp.arange(QUERIES, dtype=jnp.int32)
    onehot = (queries[:, None] == targets[None, :]).astype(jnp.float32)
    partial_scores = jnp.sum(values[:, None] * onehot, axis=0)
    scores = lax.psum(partial_scores, ("expert", "matrix"))
    return (precond[None], scores)


def solution(mesh):
    in_specs = (
        P(("layer", "expert"), None, "matrix", None),
        P("layer", None, ("expert", "matrix")),
        P("layer", ("expert", "matrix"), None),
        P("layer", ("expert", "matrix"), None),
        P(("layer", "expert")),
        P(("layer", "expert"), None),
    )
    out_specs = (P(("layer", "expert"), None, "matrix", None), P("layer"))
    return jax.shard_map(shards, mesh=mesh, in_specs=in_specs, out_specs=out_specs, check_vma=False)
```

profile of v0, /device:TPU:0, one launch (start us, length us, event | category | flops | bytes accessed | tf_op | source)
XLA Modules:
  0.0 419.3 jit_solution(11684869709950085901)
XLA Ops:
  7.2 1.4 copy.14
  8.6 21.3 %all_to_all.36 = f32[16,12,768]{2,1,0:T(8,128)S(1)} all-to-all(f32[16,12,768]{2,1,0:T(8,128)S(1)} %copy.14), channel_id=1, replica_groups=mesh['layer'=2,'expert'=16,'matrix'=4] {'expert'}, dimensions={0} | all-to-all | bytes 1179648 | tf_op jit(solution)/shard_map/all_to_all | solution.py:19
  29.9 0.9 all_to_all.31
  30.9 0.0 all-gather.6.cloned.1.call-start
  30.9 0.7 all-gather.6.cloned.1.call-update
  31.6 25.2 %all_to_all.37 = f32[16,32,768]{2,1,0:T(8,128)S(1)} all-to-all(f32[16,32,768]{2,1,0:T(8,128)S(1)} %copy-done.2), channel_id=1, replica_groups=mesh['layer'=2,'expert'=16,'matrix'=4] {'expert'}, dimensions={0} | all-to-all | bytes 3145728 | tf_op jit(solution)/shard_map/all_to_all | solution.py:18
  56.8 4.5 %all-to-all-start = ((f32[16,2048,32]{1,2,0:T(8,128)}), f32[16,2048,32]{1,2,0:T(8,128)}, u32[]{:S(2)}, u32[]{:S(2)}) async-start(f32[16,2048,32]{1,2,0:T(8,128)} %param.7), calls=%async_computation | async-start | bytes 8388608 | tf_op jit(solution)/shard_map/all_to_all | solution.py:16
  61.3 0.0 reduce-scatter.2.cloned.1.call-start
  61.4 1.3 broadcast_add_fusion
  62.7 2.4 reshape_squeeze.3
  65.1 2.0 copy.15
  67.2 2.6 reshape.33
  69.8 51.2 %all-to-all-done = f32[16,2048,32]{1,2,0:T(8,128)} async-done(((f32[16,2048,32]{1,2,0:T(8,128)}), f32[16,2048,32]{1,2,0:T(8,128)}, u32[]{:S(2)}, u32[]{:S(2)}) %all-to-all-start) | async-done | bytes 4194336 | tf_op jit(solution)/shard_map/all_to_all | solution.py:16
  121.0 9.2 %all-gather.6.cloned.1.call-done = f32[1,1,2048,768]{3,2,1,0:T(8,128)} async-done(((f32[1,1,512,768]{3,2,1,0:T(8,128)}), f32[1,1,2048,768]{3,2,1,0:T(8,128)}) %all-gather.6.cloned.1.call-update) | async-done | bytes 6291472 | tf_op jit(solution)/shard_map/all_gather | solution.py:33
  130.1 13.4 %fusion = f32[512,768]{1,0:T(8,128)S(1)} fusion(f32[2048,512]{0,1:T(8,128)} %bitcast.2, f32[1,1,2048,768]{3,2,1,0:T(8,128)} %all-gather.6.cloned.1.call-done), kind=kOutput, calls=%fused_computation | convolution fusion | flops 9663676416 | bytes 12058624 | tf_op jit(solution)/shard_map/ik,if->kf/dot_general | solution.py:30
  143.5 4.1 bitcast_divide_fusion
  147.6 4.0 fusion.3
  151.6 14.2 %convolution_bitcast_fusion = f32[2048,768]{0,1:T(8,128)} fusion(f32[512,768]{1,0:T(8,128)S(1)} %fusion.3, f32[2048,512]{0,1:T(8,128)} %bitcast.2), kind=kOutput, calls=%fused_computation.2 | convolution fusion | flops 9663676416 | bytes 12058624 | tf_op jit(solution)/shard_map/dot_general | solution.py:41
  165.8 1.4 copy-done
  167.2 0.5 copy.16
  168.9 61.7 %reduce-scatter.2.cloned.1.call-done = f32[512,768]{0,1:T(8,128)} async-done(((f32[2048,768]{0,1:T(8,128)}), f32[512,768]{0,1:T(8,128)}) %reduce-scatter.2.cloned.1.call-update) | async-done | bytes 1572880 | tf_op jit(solution)/shard_map/reduce_scatter | solution.py:43
  230.6 2.5 fusion.2
  233.1 1.6 copy.17
  235.5 177.3 %psum.7 = f32[32]{0:T(128)} all-reduce(f32[32]{0:T(128)S(1)} %compare_select_fusion), channel_id=1, replica_groups=mesh['layer'=2,'expert'=16,'matrix'=4] {'expert','matrix'}, use_global_device_ids=true, to_apply=%region_2.0 | all-reduce | flops 32 | bytes 256 | tf_op jit(solution)/shard_map/psum | solution.py:55
  (10 shorter events, 0.1 us)
Async XLA Ops:
  7.2 55.5 %all-gather.4.cloned.1.call-start = ((), (), s32[]{:S(2)}) async-start(), calls=%async_computation.4 | async-start | bytes 2949120 | tf_op jit(solution)/shard_map/all_gather | solution.py:21
  29.9 1.7 copy-start.2
  30.9 99.2 %all-gather.6.cloned.1.call-start = ((), (), s32[]{:S(2)}) async-start(), calls=%async_computation.6 | async-start | bytes 7864320 | tf_op jit(solution)/shard_map/all_gather | solution.py:33
  56.8 64.2 %all-to-all-start = ((f32[16,2048,32]{1,2,0:T(8,128)}), f32[16,2048,32]{1,2,0:T(8,128)}, u32[]{:S(2)}, u32[]{:S(2)}) async-start(f32[16,2048,32]{1,2,0:T(8,128)} %param.7), calls=%async_computation | async-start | bytes 8388608 | tf_op jit(solution)/shard_map/all_to_all | solution.py:16
  61.3 169.3 %reduce-scatter.2.cloned.1.call-start = ((), (), s32[]{:S(2)}) async-start(), calls=%async_computation.5 | async-start | bytes 7864320 | tf_op jit(solution)/shard_map/reduce_scatter | solution.py:43
  130.1 13.4 %copy-start.1 = (f32[16,32,768]{2,1,0:T(8,128)S(1)}, f32[16,32,768]{2,1,0:T(8,128)}, u32[]{:S(2)}) copy-start(f32[16,32,768]{2,1,0:T(8,128)} %broadcast_add_fusion) | copy-start | bytes 4718596
  165.8 1.4 copy-start
Sparse Core Ops, SparseCore 0:
  31.0 31.6 all-gather.3
  64.3 65.7 all-gather.5
  165.9 64.6 reduce-scatter.1
where the time goes:
time: 420 us; the launch traced here: 419 us
  blocking collectives  224 us (53%)
  waiting for transfers between devices  123 us (29%)
  matrix products  35.6 us (8%)
  between operations  15.8 us (4%)
  local copies, waits for them, and re-layouts  12.9 us (3%)
  starting transfers between devices  4.66 us (1%)
    psum x1, blocking collectives, shards(): scores = lax.psum(partial_scores, ('expert', 'matrix'))  177 us
    reduce_scatter x1, waiting for transfers between devices, shards(): lax.psum_scatter(project_one(jnp.int32(0), own_rows * lax.axis_size('matr...  61.7 us
    all_to_all x1, waiting for transfers between devices, shards(): lax.all_to_all(basis_out, 'expert', split_axis=0, concat_axis=2, tiled=True)  51.2 us
    all_to_all x1, blocking collectives, shards(): lax.all_to_all(eigvals, 'expert', split_axis=0, concat_axis=1, tiled=True)  25.2 us
    all_to_all x1, blocking collectives, shards(): lax.all_to_all(basis_in, 'expert', split_axis=0, concat_axis=1, tiled=True)  21.3 us
    dot_general x1, matrix products, project_one(): return jnp.dot(columns, back, precision=highest)  14.2 us
    dot_general x1, matrix products, shards(): jnp.einsum('ik,if->kf', columns, lax.all_gather(local_rows[0], 'matrix',...  13.4 us
    all_gather x1, waiting for transfers between devices, shards(): lax.all_gather(local_rows[0], 'matrix', axis=0, tiled=True)  9.16 us
  transfers between devices with their start and end apart: 4, of which 3 were waited for; matrix products, arithmetic and copies ran while one was open for 2% of the time, Pallas kernels for 0%

commit v1 on v0

--- a/solution.py
+++ b/solution.py
@@ -52,7 +52,7 @@
     targets = jnp.arange(QUERIES, dtype=jnp.int32)
     onehot = (queries[:, None] == targets[None, :]).astype(jnp.float32)
     partial_scores = jnp.sum(values[:, None] * onehot, axis=0)
-    scores = lax.psum(partial_scores, ("expert", "matrix"))
+    scores = lax.psum(lax.psum(partial_scores, "matrix"), "expert")
     return (precond[None], scores)
 
 

time: 420 us -> 292 us (0.70)
  blocking collectives: 224 us -> 95.7 us
    psum x1 -> x2, blocking collectives: 177 us -> 49.3 us  [shards(): scores = lax.psum(lax.psum(partial_scores, 'matrix'), 'expert')]
  transfers between devices with their start and end apart: 4 -> 4, of which waited for: 3 -> 3; matrix products, arithmetic and copies ran while one was open for 2% -> 3% of each run, Pallas kernels for 0% -> 0%
where the time goes in v1:
time: 292 us; the launch traced here: 291 us
  waiting for transfers between devices  123 us (42%)
  blocking collectives  95.7 us (33%)
  matrix products  35.5 us (12%)
  between operations  15.7 us (5%)
  local copies, waits for them, and re-layouts  12.9 us (4%)
  starting transfers between devices  4.67 us (2%)
  other arithmetic  3.77 us (1%)
    reduce_scatter x1, waiting for transfers between devices, shards(): lax.psum_scatter(project_one(jnp.int32(0), own_rows * lax.axis_size('matr...  61.7 us
    all_to_all x1, waiting for transfers between devices, shards(): lax.all_to_all(basis_out, 'expert', split_axis=0, concat_axis=2, tiled=True)  51.2 us
    psum x2, blocking collectives, shards(): scores = lax.psum(lax.psum(partial_scores, 'matrix'), 'expert')  49.3 us
    all_to_all x1, blocking collectives, shards(): lax.all_to_all(eigvals, 'expert', split_axis=0, concat_axis=1, tiled=True)  25.2 us
    all_to_all x1, blocking collectives, shards(): lax.all_to_all(basis_in, 'expert', split_axis=0, concat_axis=1, tiled=True)  21.3 us
    dot_general x1, matrix products, project_one(): return jnp.dot(columns, back, precision=highest)  14.1 us
    dot_general x1, matrix products, shards(): jnp.einsum('ik,if->kf', columns, lax.all_gather(local_rows[0], 'matrix',...  13.4 us
    all_gather x1, waiting for transfers between devices, shards(): lax.all_gather(local_rows[0], 'matrix', axis=0, tiled=True)  9.14 us
  transfers between devices with their start and end apart: 4, of which 3 were waited for; matrix products, arithmetic and copies ran while one was open for 3% of the time, Pallas kernels for 0%

profile of v1, /device:TPU:0, one launch (start us, length us, event | category | flops | bytes accessed | tf_op | source)
XLA Modules:
  0.0 291.1 jit_solution(16280962832654655030)
XLA Ops:
  7.2 1.4 copy.14
  8.6 21.3 %all_to_all.36 = f32[16,12,768]{2,1,0:T(8,128)S(1)} all-to-all(f32[16,12,768]{2,1,0:T(8,128)S(1)} %copy.14), channel_id=1, replica_groups=mesh['layer'=2,'expert'=16,'matrix'=4] {'expert'}, dimensions={0} | all-to-all | bytes 1179648 | tf_op jit(solution)/shard_map/all_to_all | solution.py:19
  29.9 0.9 all_to_all.31
  30.9 0.7 all-gather.6.cloned.1.call-update
  31.7 25.2 %all_to_all.37 = f32[16,32,768]{2,1,0:T(8,128)S(1)} all-to-all(f32[16,32,768]{2,1,0:T(8,128)S(1)} %copy-done.2), channel_id=1, replica_groups=mesh['layer'=2,'expert'=16,'matrix'=4] {'expert'}, dimensions={0} | all-to-all | bytes 3145728 | tf_op jit(solution)/shard_map/all_to_all | solution.py:18
  56.8 4.6 %all-to-all-start = ((f32[16,2048,32]{1,2,0:T(8,128)}), f32[16,2048,32]{1,2,0:T(8,128)}, u32[]{:S(2)}, u32[]{:S(2)}) async-start(f32[16,2048,32]{1,2,0:T(8,128)} %param.7), calls=%async_computation | async-start | bytes 8388608 | tf_op jit(solution)/shard_map/all_to_all | solution.py:16
  61.4 0.0 reduce-scatter.2.cloned.1.call-start
  61.4 1.3 broadcast_add_fusion
  62.7 2.4 reshape_squeeze.3
  65.2 2.0 copy.15
  67.2 2.6 reshape.33
  69.8 51.2 %all-to-all-done = f32[16,2048,32]{1,2,0:T(8,128)} async-done(((f32[16,2048,32]{1,2,0:T(8,128)}), f32[16,2048,32]{1,2,0:T(8,128)}, u32[]{:S(2)}, u32[]{:S(2)}) %all-to-all-start) | async-done | bytes 4194336 | tf_op jit(solution)/shard_map/all_to_all | solution.py:16
  121.0 9.1 %all-gather.6.cloned.1.call-done = f32[1,1,2048,768]{3,2,1,0:T(8,128)} async-done(((f32[1,1,512,768]{3,2,1,0:T(8,128)}), f32[1,1,2048,768]{3,2,1,0:T(8,128)}) %all-gather.6.cloned.1.call-update) | async-done | bytes 6291472 | tf_op jit(solution)/shard_map/all_gather | solution.py:33
  130.1 13.4 %fusion = f32[512,768]{1,0:T(8,128)S(1)} fusion(f32[2048,512]{0,1:T(8,128)} %bitcast.2, f32[1,1,2048,768]{3,2,1,0:T(8,128)} %all-gather.6.cloned.1.call-done), kind=kOutput, calls=%fused_computation | convolution fusion | flops 9663676416 | bytes 12058624 | tf_op jit(solution)/shard_map/ik,if->kf/dot_general | solution.py:30
  143.5 4.1 %bitcast_divide_fusion = f32[512,768]{1,0:T(8,128)S(1)} fusion(f32[16,32,768]{2,1,0:T(8,128)S(1)} %copy-done.1, f32[512,768]{1,0:T(8,128)S(1)} %fusion, f32[768,768]{1,0:T(8,128)S(1)} %reshape.33), kind=kOutput, calls=%fused_computation.5 | convolution fusion | flops 3624271872 | bytes 7077888 | tf_op jit(solution)/shard_map/dot_general | solution.py:36
  147.6 4.0 %fusion.3 = f32[512,768]{1,0:T(8,128)S(1)} fusion(f32[512,768]{1,0:T(8,128)S(1)} %bitcast_divide_fusion, f32[768,768]{1,0:T(8,128)S(1)} %reshape.33), kind=kOutput, calls=%fused_computation.9 | convolution fusion | flops 3623878656 | bytes 5505024 | tf_op jit(solution)/shard_map/kg,hg->kh/dot_general | solution.py:38
  151.6 14.1 %convolution_bitcast_fusion = f32[2048,768]{0,1:T(8,128)} fusion(f32[512,768]{1,0:T(8,128)S(1)} %fusion.3, f32[2048,512]{0,1:T(8,128)} %bitcast.2), kind=kOutput, calls=%fused_computation.2 | convolution fusion | flops 9663676416 | bytes 12058624 | tf_op jit(solution)/shard_map/dot_general | solution.py:41
  165.7 1.4 copy-done
  167.1 0.5 copy.16
  168.9 61.7 %reduce-scatter.2.cloned.1.call-done = f32[512,768]{0,1:T(8,128)} async-done(((f32[2048,768]{0,1:T(8,128)}), f32[512,768]{0,1:T(8,128)}) %reduce-scatter.2.cloned.1.call-update) | async-done | bytes 1572880 | tf_op jit(solution)/shard_map/reduce_scatter | solution.py:43
  230.6 2.5 fusion.2
  233.0 1.6 copy.17
  235.3 8.5 %psum.14 = f32[32]{0:T(128)S(1)} all-reduce(f32[32]{0:T(128)S(1)} %compare_select_fusion), channel_id=1, replica_groups=mesh['layer'=2,'expert'=16,'matrix'=4] {'matrix'}, use_global_device_ids=true, to_apply=%region_2.0 | all-reduce | flops 32 | bytes 256 | tf_op jit(solution)/shard_map/psum | solution.py:55
  243.8 40.8 %psum.15 = f32[32]{0:T(128)} all-reduce(f32[32]{0:T(128)S(1)} %psum.14), channel_id=1, replica_groups=mesh['layer'=2,'expert'=16,'matrix'=4] {'expert'}, use_global_device_ids=true, to_apply=%region_3.0 | all-reduce | flops 32 | bytes 256 | tf_op jit(solution)/shard_map/psum | solution.py:55
  (11 shorter events, 0.1 us)
Async XLA Ops:
  7.2 55.6 %all-gather.4.cloned.1.call-start = ((), (), s32[]{:S(2)}) async-start(), calls=%async_computation.4 | async-start | bytes 2949120 | tf_op jit(solution)/shard_map/all_gather | solution.py:21
  29.9 1.7 copy-start.2
  30.9 99.2 %all-gather.6.cloned.1.call-start = ((), (), s32[]{:S(2)}) async-start(), calls=%async_computation.6 | async-start | bytes 7864320 | tf_op jit(solution)/shard_map/all_gather | solution.py:33
  56.8 64.2 %all-to-all-start = ((f32[16,2048,32]{1,2,0:T(8,128)}), f32[16,2048,32]{1,2,0:T(8,128)}, u32[]{:S(2)}, u32[]{:S(2)}) async-start(f32[16,2048,32]{1,2,0:T(8,128)} %param.7), calls=%async_computation | async-start | bytes 8388608 | tf_op jit(solution)/shard_map/all_to_all | solution.py:16
  61.4 169.2 %reduce-scatter.2.cloned.1.call-start = ((), (), s32[]{:S(2)}) async-start(), calls=%async_computation.5 | async-start | bytes 7864320 | tf_op jit(solution)/shard_map/reduce_scatter | solution.py:43
  130.1 13.4 %copy-start.1 = (f32[16,32,768]{2,1,0:T(8,128)S(1)}, f32[16,32,768]{2,1,0:T(8,128)}, u32[]{:S(2)}) copy-start(f32[16,32,768]{2,1,0:T(8,128)} %broadcast_add_fusion) | copy-start | bytes 4718596
  165.7 1.4 copy-start
Sparse Core Ops, SparseCore 0:
  31.0 31.6 all-gather.3
  64.3 65.7 all-gather.5
  165.8 64.6 reduce-scatter.1
